TPU v7x, 32 devices: a whole 2x2x4 slice. The times are simulated.
32 devices in a mesh: zero: 8 (over y, x, core), tp: 4 (over z).
Axes of the slice: x: 2, y: 2, z: 4, core: 2. Of those that a mesh axis runs over, the one named last changes fastest.
Arguments:
- weight_gate: bfloat16 [2560, 9728], P('zero', 'tp'), may hold values from -0.125 to 0.125
- low_gate: bfloat16 [2560, 16], P('zero'), may hold values from -0.125 to 0.125
- high_gate: bfloat16 [16, 9728], P(None, 'tp'), may hold values from -1.5 to 1.5
- weight_up: bfloat16 [2560, 9728], P('zero', 'tp'), may hold values from -0.125 to 0.125
- low_up: bfloat16 [2560, 16], P('zero'), may hold values from -0.125 to 0.125
- high_up: bfloat16 [16, 9728], P(None, 'tp'), may hold values from -1.5 to 1.5
- weight_down: bfloat16 [9728, 2560], P('tp', 'zero'), may hold values from -0.0625 to 0.0625
- low_down: bfloat16 [9728, 16], P('tp'), may hold values from -0.0625 to 0.0625
- high_down: bfloat16 [16, 2560], P(None, 'zero'), may hold values from -1.5 to 1.5
- norm_train: float32 [2560], P(('zero', 'tp')), may hold values from 0.25 to 1.75
- norm_step: float32 [2560], P(('zero', 'tp')), may hold values from -0.3 to 0.3
Outputs:
- ready_gate: bfloat16 [2560, 9728], P(None, 'tp')
- ready_up: bfloat16 [2560, 9728], P(None, 'tp')
- ready_down: bfloat16 [9728, 2560], P('tp')
- serve_norm: bfloat16 [2560], replicated
All inputs are finite; a program needn't handle non-finite values.
Results may differ from a plain program's by a relative error of at most 0.001.
Values may be sent and summed in bfloat16 or wider, within the bound.
A program may use at most 128 MiB of HBM per device.

v0:
```python
import jax
import jax.numpy as jnp
from jax import lax
from jax.sharding import PartitionSpec as P

mix_rate = 0.5


def local(
    weight_gate,
    low_gate,
    high_gate,
    weight_up,
    low_up,
    high_up,
    weight_down,
    low_down,
    high_down,
    norm_train,
    norm_step,
):
    moved_gate, moved_up, moved_down, factor_gate, factor_up, factor_down = (
        lax.all_gather(weight_gate, "zero", axis=0, tiled=True),
        lax.all_gather(weight_up, "zero", axis=0, tiled=True),
        lax.all_gather(weight_down, "zero", axis=1, tiled=True),
        lax.all_gather(low_gate, "zero", axis=0, tiled=True),
        lax.all_gather(low_up, "zero", axis=0, tiled=True),
        lax.all_gather(high_down, "zero", axis=1, tiled=True),
    )
    latest_gate = moved_gate.astype(jnp.float32) + mix_rate * jnp.dot(
        factor_gate, high_gate, preferred_element_type=jnp.float32
    )
    ready_gate = latest_gate.astype(jnp.bfloat16)
    latest_up = moved_up.astype(jnp.float32) + mix_rate * jnp.dot(
        factor_up, high_up, preferred_element_type=jnp.float32
    )
    ready_up = latest_up.astype(jnp.bfloat16)
    latest_down = moved_down.astype(jnp.float32) + mix_rate * jnp.dot(
        low_down, factor_down, preferred_element_type=jnp.float32
    )
    ready_down = latest_down.astype(jnp.bfloat16)
    serve_norm = lax.all_gather(
        (norm_train + norm_step).astype(jnp.bfloat16), ("zero", "tp"), axis=0, tiled=True
    )
    return (ready_gate, ready_up, ready_down, serve_norm)


def solution(mesh):
    return jax.shard_map(
        local,
        mesh=mesh,
        in_specs=(
            P("zero", "tp"),
            P("zero", None),
            P(None, "tp"),
            P("zero", "tp"),
            P("zero", None),
            P(None, "tp"),
            P("tp", "zero"),
            P("tp", None),
            P(None, "zero"),
            P(("zero", "tp")),
            P(("zero", "tp")),
        ),
        out_specs=(P(None, "tp"), P(None, "tp"), P("tp", None), P()),
        check_vma=False,
    )
```

profile of v0, /device:TPU:0, one launch (start us, length us, event | category | flops | bytes accessed | tf_op | source)
XLA Modules:
  0.0 248.3 jit_solution(13862826156925674627)
XLA Ops:
  7.2 0.0 copy-start
  7.2 0.0 all-gather.11.cloned.1.call-start
  7.2 0.7 all-gather.11.cloned.1.call-update
  7.9 0.0 all-gather.7.cloned.1.call-start
  8.0 0.7 all-gather.7.cloned.1.call-update
  8.7 0.0 all-gather.9.cloned.1.call-start
  8.7 0.7 all-gather.9.cloned.1.call-update
  9.4 10.9 %all-gather = bf16[8,320,16]{1,2,0:T(8,128)(2,1)S(1)} all-gather(bf16[1,320,16]{1,2,0:T(8,128)(2,1)} %bitcast.17), channel_id=1, replica_groups=mesh['zero'=8,'tp'=4] {'zero'}, dimensions={0}, use_global_device_ids=true | all-gather | bytes 92160 | tf_op jit(solution)/shard_map/all_gather | solution.py:26
  20.3 0.1 reshape.11
  20.4 9.6 %all-gather.1 = bf16[8,320,16]{1,2,0:T(8,128)(2,1)S(1)} all-gather(bf16[1,320,16]{1,2,0:T(8,128)(2,1)} %bitcast.18), channel_id=1, replica_groups=mesh['zero'=8,'tp'=4] {'zero'}, dimensions={0}, use_global_device_ids=true | all-gather | bytes 92160 | tf_op jit(solution)/shard_map/all_gather | solution.py:27
  30.0 0.1 reshape.13
  30.1 9.0 %all-gather.2 = bf16[8,320,16]{1,2,0:T(8,128)(2,1)S(1)} all-gather(bf16[1,320,16]{1,2,0:T(8,128)(2,1)} %bitcast.19), channel_id=1, replica_groups=mesh['zero'=8,'tp'=4] {'zero'}, dimensions={0}, use_global_device_ids=true | all-gather | bytes 92160 | tf_op jit(solution)/shard_map/all_gather | solution.py:28
  39.2 0.1 reshape.15
  39.3 0.7 add_convert_fusion.3
  40.0 0.2 dynamic-update-slice
  40.2 40.8 %all-reduce = bf16[2560]{0:T(1024)(128)(2,1)} all-reduce(bf16[2560]{0:T(1024)(128)(2,1)S(1)} %dynamic-update-slice), channel_id=1, replica_groups=mesh['zero'=8,'tp'=4] {'zero','tp'}, use_global_device_ids=true, to_apply=%add | all-reduce | flops 2560 | bytes 10240
  81.0 4.8 %all-gather.11.cloned.1.call-done = bf16[2432,2560]{0,1:T(8,128)(2,1)} async-done(((bf16[2432,320]{0,1:T(8,128)(2,1)}), bf16[2432,2560]{0,1:T(8,128)(2,1)}) %all-gather.11.cloned.1.call-update) | async-done | bytes 12451856 | tf_op jit(solution)/shard_map/all_gather | solution.py:25
  85.8 17.3 %copy.22 = bf16[2432,2560]{1,0:T(8,128)(2,1)} copy(bf16[2432,2560]{0,1:T(8,128)(2,1)} %all-gather.11.cloned.1.call-done) | data formatting | bytes 24903680 | tf_op jit(solution)/shard_map/all_gather | solution.py:25
  103.0 0.0 copy-done
  103.0 0.0 copy-start.2
  103.0 9.4 %add_convert_fusion = bf16[2432,2560]{1,0:T(8,128)(2,1)} fusion(bf16[2432,2560]{1,0:T(8,128)(2,1)} %copy.22, bf16[2432,16]{0,1:T(8,128)(2,1)S(1)} %copy-done, bf16[2560,16]{0,1:T(8,128)(2,1)S(1)} %reshape.15), kind=kOutput, calls=%fused_computation | convolution fusion | flops 224133120 | bytes 25063424 | tf_op jit(solution)/shard_map/dot_general | solution.py:38
  112.4 0.0 copy-start.3
  112.4 46.7 %all-gather.7.cloned.1.call-done = bf16[2560,2432]{1,0:T(8,128)(2,1)} async-done(((bf16[320,2432]{1,0:T(8,128)(2,1)}), bf16[2560,2432]{1,0:T(8,128)(2,1)}) %all-gather.7.cloned.1.call-update) | async-done | bytes 12451856 | tf_op jit(solution)/shard_map/all_gather | solution.py:23
  159.1 0.0 copy-done.2
  159.1 0.0 copy-start.1
  159.1 9.4 %add_convert_fusion.2 = bf16[2560,2432]{1,0:T(8,128)(2,1)} fusion(bf16[2560,2432]{1,0:T(8,128)(2,1)} %all-gather.7.cloned.1.call-done, bf16[2560,16]{0,1:T(8,128)(2,1)S(1)} %reshape.11, bf16[16,2432]{1,0:T(8,128)(2,1)S(1)} %copy-done.2), kind=kOutput, calls=%fused_computation.2 | convolution fusion | flops 224133120 | bytes 25063424 | tf_op jit(solution)/shard_map/dot_general | solution.py:30
  168.4 64.0 %all-gather.9.cloned.1.call-done = bf16[2560,2432]{1,0:T(8,128)(2,1)} async-done(((bf16[320,2432]{1,0:T(8,128)(2,1)}), bf16[2560,2432]{1,0:T(8,128)(2,1)}) %all-gather.9.cloned.1.call-update) | async-done | bytes 12451856 | tf_op jit(solution)/shard_map/all_gather | solution.py:24
  232.4 0.0 copy-done.3
  232.4 9.3 %add_convert_fusion.1 = bf16[2560,2432]{1,0:T(8,128)(2,1)} fusion(bf16[2560,2432]{1,0:T(8,128)(2,1)} %all-gather.9.cloned.1.call-done, bf16[2560,16]{0,1:T(8,128)(2,1)S(1)} %reshape.13, bf16[16,2432]{1,0:T(8,128)(2,1)S(1)} %copy-done.3), kind=kOutput, calls=%fused_computation.1 | convolution fusion | flops 224133120 | bytes 25063424 | tf_op jit(solution)/shard_map/dot_general | solution.py:34
  241.8 0.0 copy-done.1
  (4 shorter events, 0.1 us)
Async XLA Ops:
  7.2 95.9 %copy-start = (bf16[2432,16]{0,1:T(8,128)(2,1)S(1)}, bf16[2432,16]{0,1:T(8,128)(2,1)}, u32[]{:S(2)}) copy-start(bf16[2432,16]{0,1:T(8,128)(2,1)} %param.18) | copy-start | bytes 233476
  7.2 78.6 %all-gather.11.cloned.1.call-start = ((), (), s32[]{:S(2)}) async-start(), calls=%async_computation.2 | async-start | bytes 14008320 | tf_op jit(solution)/shard_map/all_gather | solution.py:25
  7.9 151.1 %all-gather.7.cloned.1.call-start = ((), (), s32[]{:S(2)}) async-start(), calls=%async_computation | async-start | bytes 14008320 | tf_op jit(solution)/shard_map/all_gather | solution.py:23
  8.7 223.8 %all-gather.9.cloned.1.call-start = ((), (), s32[]{:S(2)}) async-start(), calls=%async_computation.1 | async-start | bytes 14008320 | tf_op jit(solution)/shard_map/all_gather | solution.py:24
  103.0 56.0 %copy-start.2 = (bf16[16,2432]{1,0:T(8,128)(2,1)S(1)}, bf16[16,2432]{1,0:T(8,128)(2,1)}, u32[]{:S(2)}) copy-start(bf16[16,2432]{1,0:T(8,128)(2,1)} %param.13) | copy-start | bytes 233476
  112.4 120.0 %copy-start.3 = (bf16[16,2432]{1,0:T(8,128)(2,1)S(1)}, bf16[16,2432]{1,0:T(8,128)(2,1)}, u32[]{:S(2)}) copy-start(bf16[16,2432]{1,0:T(8,128)(2,1)} %param.16) | copy-start | bytes 233476
  159.1 82.7 %copy-start.1 = (bf16[2432,16]{0,1:T(8,128)(2,1)S(1)}, bf16[2432,16]{0,1:T(8,128)(2,1)}, u32[]{:S(2)}) copy-start(bf16[2432,16]{0,1:T(8,128)(2,1)} %param.18) | copy-start | bytes 233476
Sparse Core Ops, SparseCore 0:
  9.9 75.8 all-gather.10
  87.6 71.3 all-gather.6
  161.0 71.4 all-gather.8
where the time goes:
time: 249 us; the launch traced here: 248 us
  waiting for transfers between devices  117 us (47%)
  blocking collectives  70.3 us (28%)
  matrix products  28.1 us (11%)
  local copies, waits for them, and re-layouts  17.9 us (7%)
  between operations  13.8 us (6%)
    all_gather x1, waiting for transfers between devices, local(): lax.all_gather(weight_up, 'zero', axis=0, tiled=True)  64 us
    all_gather x1, waiting for transfers between devices, local(): lax.all_gather(weight_gate, 'zero', axis=0, tiled=True)  46.7 us
    unnamed x1, blocking collectives  40.8 us
    all_gather x1, local copies, waits for them, and re-layouts, local(): lax.all_gather(weight_down, 'zero', axis=1, tiled=True)  17.3 us
    all_gather x1, blocking collectives, local(): lax.all_gather(low_gate, 'zero', axis=0, tiled=True)  10.9 us
    all_gather x1, blocking collectives, local(): lax.all_gather(low_up, 'zero', axis=0, tiled=True)  9.56 us
    dot_general x1, matrix products, local(): jnp.dot(low_down, factor_down, preferred_element_type=jnp.float32)  9.37 us
    dot_general x1, matrix products, local(): jnp.dot(factor_gate, high_gate, preferred_element_type=jnp.float32)  9.36 us
  transfers between devices with their start and end apart: 3, of which 3 were waited for; matrix products, arithmetic and copies ran while one was open for 15% of the time, Pallas kernels for 0%

commit v1 on v0

v1 whole, which is shorter than its diff:
```python
import functools

import jax
import jax.numpy as jnp
from jax import lax
from jax.experimental import pallas as pl
from jax.experimental.pallas import tpu as pltpu
from jax.sharding import PartitionSpec as P

mix_rate = 0.5
MESH = pl.DeviceIdType.MESH
LANES = 128
CHUNKS = 4
GROUP = 8


def merge_rows(weight, factor, other):
    product = lax.dot_general(
        factor, other, (((0,), (0,)), ((), ())), preferred_element_type=jnp.float32
    )
    return (weight.astype(jnp.float32) + mix_rate * product).astype(jnp.bfloat16)


def gather_kernel(
    weight_down, factor_down, other_down,
    weight_gate, factor_gate, other_gate,
    weight_up, factor_up, other_up,
    gate, up, down, held,
    x_send, x_recv, y_send, y_recv, fx_send, fx_recv, fy_send, fy_recv, p_send, p_recv,
):
    rows, columns = weight_gate.shape
    step = rows // CHUNKS
    half = CHUNKS // 2
    me = lax.axis_index("zero")
    core = lax.rem(me, 2)
    x = lax.rem(lax.div(me, 2), 2)
    y = lax.div(me, 4)

    def at(yy, xx, cc):
        return (yy * 2 + xx) * 2 + cc

    partner = at(y, x, 1 - core)
    across_x = at(y, 1 - x, core)
    across_y = at(1 - y, x, core)
    across = at(1 - y, 1 - x, core)

    barrier = pltpu.get_barrier_semaphore()
    for peer in (partner, across_x, across_y):
        pl.semaphore_signal(barrier, inc=1, device_id={"zero": peer}, device_id_type=MESH)
    pl.semaphore_wait(barrier, 3)

    stacks = (held, gate, up)
    sources = (
        (weight_down, factor_down, other_down),
        (weight_gate, factor_gate, other_gate),
        (weight_up, factor_up, other_up),
    )

    def part(i, owner, c, count=1):
        first = pl.multiple_of(owner * rows + c * step, 16)
        return stacks[i].at[pl.ds(first, step * count), :]

    def copy(i, owner, c, peer, send, recv, count=1):
        ref = part(i, owner, c, count)
        return pltpu.make_async_remote_copy(
            src_ref=ref, dst_ref=ref, send_sem=send, recv_sem=recv,
            device_id={"zero": peer}, device_id_type=MESH,
        )

    def on_x(i, owner, c):
        return copy(i, owner, c, across_x, x_send.at[i, c], x_recv.at[i, c])

    def on_y(i, owner, c):
        return copy(i, owner, c, across_y, y_send.at[i, c], y_recv.at[i, c])

    def forward_x(i, owner, c):
        return copy(i, owner, c, across_x, fx_send.at[i, c - half], fx_recv.at[i, c - half])

    def forward_y(i, owner, c):
        return copy(i, owner, c, across_y, fy_send.at[i, c], fy_recv.at[i, c])

    def share(i, slot, owner, c):
        return copy(i, owner, c, partner, p_send.at[slot, i, c], p_recv.at[slot, i, c])

    early, late = range(half), range(half, CHUNKS)
    sent = []

    def go(dma):
        dma.start()
        sent.append(dma)

    for i in range(3):
        weight, factor, other = sources[i]
        first = pl.multiple_of(me * rows, 16)

        @pl.loop(0, columns // LANES)
        def _(t):
            cols = pl.ds(pl.multiple_of(t * LANES, LANES), LANES)
            stacks[i][pl.ds(first, rows), cols] = merge_rows(
                weight[:, cols], factor[...], other[:, cols]
            )

        for cx, cy in zip((*early, *late), (*late, *early)):
            go(on_x(i, me, cx))
            go(on_y(i, me, cy))
        for c in range(CHUNKS):
            go(share(i, 0, me, c))

    def turn(owner):
        base = pl.multiple_of(lax.div(owner, 2) * (2 * rows), LANES)

        @pl.loop(0, columns // LANES)
        def _(t):
            cols = pl.ds(pl.multiple_of(t * LANES, LANES), LANES)
            down[cols, pl.ds(base, 2 * rows)] = held[pl.ds(base, 2 * rows), cols].T

    def shared(i, slot, owner):
        other_core = owner + partner - me
        for c in range(CHUNKS):
            share(i, slot, other_core, c).wait_recv()

    for i in range(3):
        for c, d in zip(early, late):
            on_x(i, across_x, c).wait_recv()
            go(forward_y(i, across_x, c))
            go(share(i, 1, across_x, c))
            on_y(i, across_y, d).wait_recv()
            go(forward_x(i, across_y, d))
            go(share(i, 2, across_y, d))
        for c, d in zip(early, late):
            on_x(i, across_x, d).wait_recv()
            go(share(i, 1, across_x, d))
            on_y(i, across_y, c).wait_recv()
            go(share(i, 2, across_y, c))
        for slot, owner in ((0, me), (1, across_x), (2, across_y)):
            shared(i, slot, owner)
            if i == 0:
                turn(owner)
    for i in range(3):
        for c, d in zip(early, late):
            forward_y(i, across, c).wait_recv()
            go(share(i, 3, across, c))
            forward_x(i, across, d).wait_recv()
            go(share(i, 3, across, d))
        if i == 0:
            shared(i, 3, across)
            turn(across)
    for i in (1, 2):
        shared(i, 3, across)
    for dma in sent:
        dma.wait_send()


def gather(sources, names):
    rows, columns = sources[0].shape
    stack = (rows * GROUP, columns)
    turned = (columns, rows * GROUP)
    dma = pltpu.SemaphoreType.DMA
    half = CHUNKS // 2
    return pl.pallas_call(
        gather_kernel,
        out_shape=(
            pltpu.VMEM(stack, jnp.bfloat16),
            pltpu.VMEM(stack, jnp.bfloat16),
            pltpu.VMEM(turned, jnp.bfloat16),
        ),
        in_specs=[pl.BlockSpec(memory_space=pltpu.VMEM)] * 9,
        out_specs=[pl.BlockSpec(memory_space=pltpu.VMEM)] * 3,
        scratch_shapes=[
            pltpu.VMEM(stack, jnp.bfloat16),
            dma((3, CHUNKS)), dma((3, CHUNKS)), dma((3, CHUNKS)), dma((3, CHUNKS)),
            dma((3, half)), dma((3, half)), dma((3, half)), dma((3, half)),
            dma((4, 3, CHUNKS)), dma((4, 3, CHUNKS)),
        ],
        compiler_params=pltpu.CompilerParams(
            collective_id=0, has_side_effects=True, vmem_limit_bytes=20 * 2**20
        ),
        name="gather_merged",
    )(*sources)


def store_kernel(gate, up, down, gate_out, up_out, down_out, sems):
    pieces = 4
    copies = []
    for i, (src, dst) in enumerate(((gate, gate_out), (up, up_out), (down, down_out))):
        size = src.shape[0] // pieces
        for k in range(pieces):
            at = pl.ds(k * size, size)
            copies.append(pltpu.make_async_copy(src.at[at, :], dst.at[at, :], sems.at[i, k]))
            copies[-1].start()
    for copy in copies:
        copy.wait()


def store(gate, up, down):
    return pl.pallas_call(
        store_kernel,
        out_shape=tuple(jax.ShapeDtypeStruct(a.shape, a.dtype) for a in (gate, up, down)),
        in_specs=[pl.BlockSpec(memory_space=pltpu.VMEM)] * 3,
        out_specs=[pl.BlockSpec(memory_space=pl.ANY)] * 3,
        scratch_shapes=[pltpu.SemaphoreType.DMA((3, 4))],
        compiler_params=pltpu.CompilerParams(vmem_limit_bytes=2**20),
        name="store_merged",
    )(gate, up, down)


def local(
    weight_gate, low_gate, high_gate,
    weight_up, low_up, high_up,
    weight_down, low_down, high_down,
    norm_train, norm_step,
    *, fast,
):
    serve_norm = lax.all_gather(
        (norm_train + norm_step).astype(jnp.bfloat16), ("zero", "tp"), axis=0, tiled=True
    )
    sources = (
        (weight_down.T, high_down, low_down.T),
        (weight_gate, low_gate.T, high_gate),
        (weight_up, low_up.T, high_up),
    )
    if fast:
        ready_gate, ready_up, ready_down = store(*gather(sum(sources, ()), None))
    else:
        down, gate, up = (merge_rows(*s) for s in sources)
        ready_gate, ready_up, ready_down = (
            lax.all_gather(a, "zero", axis=0, tiled=True) for a in (gate, up, down)
        )
        ready_down = ready_down.T
    return (ready_gate, ready_up, ready_down, serve_norm)


def solution(mesh):
    def step(*args):
        zero, tp = mesh.shape["zero"], mesh.shape["tp"]
        rows, columns = args[0].shape[0] // zero, args[0].shape[1] // tp
        fast = (
            zero == GROUP
            and rows % (16 * CHUNKS) == 0
            and columns % LANES == 0
            and args[6].shape == args[0].shape[::-1]
        )
        return jax.shard_map(
            functools.partial(local, fast=fast),
            mesh=mesh,
            in_specs=(
                P("zero", "tp"), P("zero", None), P(None, "tp"),
                P("zero", "tp"), P("zero", None), P(None, "tp"),
                P("tp", "zero"), P("tp", None), P(None, "zero"),
                P(("zero", "tp")), P(("zero", "tp")),
            ),
            out_specs=(P(None, "tp"), P(None, "tp"), P("tp", None), P()),
            check_vma=False,
        )(*args)

    return step
```

time: 249 us -> 237 us (0.952)
  Pallas kernels: 0 us -> 177 us
  waiting for transfers between devices: 117 us -> 0 us
  blocking collectives: 70.3 us -> 39.6 us
  matrix products: 28.1 us -> 0 us
  between operations: 13.8 us -> 0.7 us
    pallas_call x0 -> x2, Pallas kernels: none -> 177 us  [the longest x1 165 us: gather(): pl.pallas_call(gather_kernel, out_shape=(pltpu.VMEM(stack, jnp.bfloat16),...]
    all_gather x3 -> x0, waiting for transfers between devices: 115 us -> none  [the longest x1 64 us: local(): lax.all_gather(weight_up, 'zero', axis=0, tiled=True)]
    all_gather x3 -> x0, blocking collectives: 29.5 us -> none  [the longest x1 10.9 us: local(): lax.all_gather(low_gate, 'zero', axis=0, tiled=True)]
    dot_general x3 -> x0, matrix products: 28.1 us -> none  [the longest x1 9.37 us: local(): jnp.dot(low_down, factor_down, preferred_element_type=jnp.float32)]
    unnamed x13 -> x14, local copies, waits for them, and re-layouts: 0.59 us -> 18.8 us
    all_gather x4 -> x0, local copies, waits for them, and re-layouts: 17.3 us -> none  [the longest x1 17.3 us: local(): lax.all_gather(weight_down, 'zero', axis=1, tiled=True)]
  transfers between devices with their start and end apart: 3 -> 0, of which waited for: 3 -> 0; matrix products, arithmetic and copies ran while one was open for 15% -> 0% of each run, Pallas kernels for 0% -> 0%
where the time goes in v1:
time: 237 us; the launch traced here: 236 us
  Pallas kernels  177 us (75%)
  blocking collectives  39.6 us (17%)
  local copies, waits for them, and re-layouts  18.8 us (8%)
    pallas_call x1, Pallas kernels, gather(): pl.pallas_call(gather_kernel, out_shape=(pltpu.VMEM(stack, jnp.bfloat16),...  165 us
    unnamed x1, blocking collectives  39.6 us
    unnamed x14, local copies, waits for them, and re-layouts  18.8 us
    pallas_call x1, Pallas kernels, store(): pl.pallas_call(store_kernel, out_shape=tuple((jax.ShapeDtypeStruct(a.shap...  12.2 us

profile of v1, /device:TPU:0, one launch (start us, length us, event | category | flops | bytes accessed | tf_op | source)
XLA Modules:
  0.0 236.3 jit_solution(9376997065966880046)
XLA Ops:
  0.6 164.9 %gather_merged.1 = (bf16[2560,2432]{1,0:T(8,128)(2,1)S(1)}, bf16[2560,2432]{1,0:T(8,128)(2,1)S(1)}, bf16[2432,2560]{1,0:T(8,128)(2,1)S(1)}) custom-call(bf16[320,2432]{1,0:T(8,128)(2,1)} %bitcast.4, bf16[16,320]{1,0:T(8,128)(2,1)} %factor_down.1, bf16[16,2432]{1,0:T(8,128)(2,1)} %bitcast.5, bf16[320,2432]{1,0:T(8,128)(2,1)} %weight_gate.1, ...), custom_call_target="tpu_custom_call" | custom-call | tf_op jit(solution)/shard_map/gather_merged/pallas_call | solution.py:160
  165.6 0.0 copy-start
  165.6 4.7 %copy-done = bf16[2560,2432]{1,0:T(8,128)(2,1)} copy-done((bf16[2560,2432]{1,0:T(8,128)(2,1)}, bf16[2560,2432]{1,0:T(8,128)(2,1)S(1)}, u32[]{:S(2)}) %copy-start) | copy-done | bytes 12451864
  170.3 0.0 copy-start.2
  170.3 4.7 %copy-done.2 = bf16[2560,2432]{1,0:T(8,128)(2,1)} copy-done((bf16[2560,2432]{1,0:T(8,128)(2,1)}, bf16[2560,2432]{1,0:T(8,128)(2,1)S(1)}, u32[]{:S(2)}) %copy-start.2) | copy-done | bytes 12451864
  175.1 0.0 copy-start.1
  175.1 4.5 %copy-done.1 = bf16[2560,2432]{1,0:T(8,128)(2,1)S(1)} copy-done((bf16[2560,2432]{1,0:T(8,128)(2,1)S(1)}, bf16[2560,2432]{1,0:T(8,128)(2,1)}, u32[]{:S(2)}) %copy-start.1) | copy-done | bytes 12451864
  179.6 0.0 copy-start.3
  179.6 4.5 %copy-done.3 = bf16[2560,2432]{1,0:T(8,128)(2,1)S(1)} copy-done((bf16[2560,2432]{1,0:T(8,128)(2,1)S(1)}, bf16[2560,2432]{1,0:T(8,128)(2,1)}, u32[]{:S(2)}) %copy-start.3) | copy-done | bytes 12451864
  184.1 0.0 copy-start.4
  184.1 0.0 copy-start.5
  184.1 12.2 %store_merged.1 = (bf16[2560,2432]{1,0:T(8,128)(2,1)}, bf16[2560,2432]{1,0:T(8,128)(2,1)}, bf16[2432,2560]{1,0:T(8,128)(2,1)}) custom-call(bf16[2560,2432]{1,0:T(8,128)(2,1)S(1)} %copy-done.1, bf16[2560,2432]{1,0:T(8,128)(2,1)S(1)} %copy-done.3, bf16[2432,2560]{1,0:T(8,128)(2,1)S(1)} %get-tuple-element.12.down), custom_call_target="tpu_custom_call" | custom-call | tf_op jit(solution)/shard_map/store_merged/pallas_call | solution.py:196
  196.4 0.0 copy-done.4
  196.4 0.0 copy-done.5
  196.4 0.2 dynamic-update-slice
  196.7 39.6 %all-reduce = bf16[2560]{0:T(1024)(128)(2,1)} all-reduce(bf16[2560]{0:T(1024)(128)(2,1)S(1)} %dynamic-update-slice), channel_id=1, replica_groups=mesh['zero'=8,'tp'=4] {'zero','tp'}, use_global_device_ids=true, to_apply=%add | all-reduce | flops 2560 | bytes 10240
  (2 shorter events, 0.0 us)
Async XLA Ops:
  165.6 4.7 %copy-start = (bf16[2560,2432]{1,0:T(8,128)(2,1)}, bf16[2560,2432]{1,0:T(8,128)(2,1)S(1)}, u32[]{:S(2)}) copy-start(bf16[2560,2432]{1,0:T(8,128)(2,1)S(1)} %get-tuple-element.10.gate) | copy-start | bytes 37355524
  170.3 4.7 %copy-start.2 = (bf16[2560,2432]{1,0:T(8,128)(2,1)}, bf16[2560,2432]{1,0:T(8,128)(2,1)S(1)}, u32[]{:S(2)}) copy-start(bf16[2560,2432]{1,0:T(8,128)(2,1)S(1)} %get-tuple-element.11.up) | copy-start | bytes 37355524
  175.1 4.5 %copy-start.1 = (bf16[2560,2432]{1,0:T(8,128)(2,1)S(1)}, bf16[2560,2432]{1,0:T(8,128)(2,1)}, u32[]{:S(2)}) copy-start(bf16[2560,2432]{1,0:T(8,128)(2,1)} %copy-done) | copy-start | bytes 37355524
  179.6 4.5 %copy-start.3 = (bf16[2560,2432]{1,0:T(8,128)(2,1)S(1)}, bf16[2560,2432]{1,0:T(8,128)(2,1)}, u32[]{:S(2)}) copy-start(bf16[2560,2432]{1,0:T(8,128)(2,1)} %copy-done.2) | copy-start | bytes 37355524
  184.1 12.2 %copy-start.4 = (f32[80]{0:T(128)S(1)}, f32[80]{0:T(128)}, u32[]{:S(2)}) copy-start(f32[80]{0:T(128)} %param.20) | copy-start | bytes 964
  184.1 12.3 %copy-start.5 = (f32[80]{0:T(128)S(1)}, f32[80]{0:T(128)}, u32[]{:S(2)}) copy-start(f32[80]{0:T(128)} %param.21) | copy-start | bytes 964

commit v2 on v1

--- a/solution.py
+++ b/solution.py
@@ -22,10 +22,13 @@
 
 
 def gather_kernel(
+    tp,
     weight_down, factor_down, other_down,
     weight_gate, factor_gate, other_gate,
     weight_up, factor_up, other_up,
-    gate, up, down, held,
+    norm_train, norm_step,
+    gate, up, down, gains, stack, turned, out_sems,
+    n_send, n_recv,
     x_send, x_recv, y_send, y_recv, fx_send, fx_recv, fy_send, fy_recv, p_send, p_recv,
 ):
     rows, columns = weight_gate.shape
@@ -44,12 +47,22 @@
     across_y = at(1 - y, x, core)
     across = at(1 - y, 1 - x, core)
 
+    mine = lax.axis_index("tp")
+    peers, width = [], 1
+    while width < tp:
+        bit = lax.rem(lax.div(mine, width), 2)
+        peers.append({"tp": mine + width - 2 * width * bit})
+        width *= 2
+    peers += [{"zero": partner}, {"zero": across_x}, {"zero": across_y}]
+
     barrier = pltpu.get_barrier_semaphore()
-    for peer in (partner, across_x, across_y):
-        pl.semaphore_signal(barrier, inc=1, device_id={"zero": peer}, device_id_type=MESH)
-    pl.semaphore_wait(barrier, 3)
-
-    stacks = (held, gate, up)
+    for peer in peers:
+        pl.semaphore_signal(barrier, inc=1, device_id=peer, device_id_type=MESH)
+    place = me * tp + mine
+    size = norm_train.shape[1]
+    gains[place, :, 0:size] = norm_train[...] + norm_step[...]
+    pl.semaphore_wait(barrier, len(peers))
+
     sources = (
         (weight_down, factor_down, other_down),
         (weight_gate, factor_gate, other_gate),
@@ -58,7 +71,7 @@
 
     def part(i, owner, c, count=1):
         first = pl.multiple_of(owner * rows + c * step, 16)
-        return stacks[i].at[pl.ds(first, step * count), :]
+        return stack.at[i, pl.ds(first, step * count), :]
 
     def copy(i, owner, c, peer, send, recv, count=1):
         ref = part(i, owner, c, count)
@@ -96,7 +109,7 @@
         @pl.loop(0, columns // LANES)
         def _(t):
             cols = pl.ds(pl.multiple_of(t * LANES, LANES), LANES)
-            stacks[i][pl.ds(first, rows), cols] = merge_rows(
+            stack[i, pl.ds(first, rows), cols] = merge_rows(
                 weight[:, cols], factor[...], other[:, cols]
             )
 
@@ -106,18 +119,41 @@
         for c in range(CHUNKS):
             go(share(i, 0, me, c))
 
-    def turn(owner):
+    for k, peer in enumerate(peers):
+        width = 1 << k
+        block = gains.at[pl.ds(lax.div(place, width) * width, width)]
+        dma = pltpu.make_async_remote_copy(
+            src_ref=block, dst_ref=block, send_sem=n_send.at[k], recv_sem=n_recv.at[k],
+            device_id=peer, device_id_type=MESH,
+        )
+        dma.start()
+        dma.wait_recv()
+        sent.append(dma)
+
+    outs = []
+
+    def put(i, slot, owner):
         base = pl.multiple_of(lax.div(owner, 2) * (2 * rows), LANES)
-
-        @pl.loop(0, columns // LANES)
-        def _(t):
-            cols = pl.ds(pl.multiple_of(t * LANES, LANES), LANES)
-            down[cols, pl.ds(base, 2 * rows)] = held[pl.ds(base, 2 * rows), cols].T
+        both = pl.ds(base, 2 * rows)
+        if i == 0:
+
+            @pl.loop(0, columns // LANES)
+            def _(t):
+                cols = pl.ds(pl.multiple_of(t * LANES, LANES), LANES)
+                turned[cols, both] = stack[0, both, cols].T
+
+            src, dst = turned.at[:, both], down.at[:, both]
+        else:
+            src, dst = stack.at[i, both, :], (gate, up)[i - 1].at[both, :]
+        dma = pltpu.make_async_copy(src, dst, out_sems.at[i, slot])
+        dma.start()
+        outs.append(dma)
 
     def shared(i, slot, owner):
         other_core = owner + partner - me
         for c in range(CHUNKS):
             share(i, slot, other_core, c).wait_recv()
+        put(i, slot, owner)
 
     for i in range(3):
         for c, d in zip(early, late):
@@ -134,74 +170,51 @@
             go(share(i, 2, across_y, c))
         for slot, owner in ((0, me), (1, across_x), (2, across_y)):
             shared(i, slot, owner)
-            if i == 0:
-                turn(owner)
     for i in range(3):
         for c, d in zip(early, late):
             forward_y(i, across, c).wait_recv()
             go(share(i, 3, across, c))
             forward_x(i, across, d).wait_recv()
             go(share(i, 3, across, d))
-        if i == 0:
-            shared(i, 3, across)
-            turn(across)
-    for i in (1, 2):
         shared(i, 3, across)
     for dma in sent:
         dma.wait_send()
-
-
-def gather(sources, names):
+    for dma in outs:
+        dma.wait()
+
+
+def gather(sources, norms, tp):
     rows, columns = sources[0].shape
     stack = (rows * GROUP, columns)
     turned = (columns, rows * GROUP)
     dma = pltpu.SemaphoreType.DMA
     half = CHUNKS // 2
+    stages = (GROUP * tp).bit_length() - 1
     return pl.pallas_call(
-        gather_kernel,
+        functools.partial(gather_kernel, tp),
         out_shape=(
-            pltpu.VMEM(stack, jnp.bfloat16),
-            pltpu.VMEM(stack, jnp.bfloat16),
+            jax.ShapeDtypeStruct(stack, jnp.bfloat16),
+            jax.ShapeDtypeStruct(stack, jnp.bfloat16),
+            jax.ShapeDtypeStruct(turned, jnp.bfloat16),
+            jax.ShapeDtypeStruct((GROUP * tp, 1, LANES), jnp.float32),
+        ),
+        in_specs=[pl.BlockSpec(memory_space=pltpu.VMEM)] * 11,
+        out_specs=[pl.BlockSpec(memory_space=pl.ANY)] * 3
+        + [pl.BlockSpec(memory_space=pltpu.VMEM)],
+        scratch_shapes=[
+            pltpu.VMEM((3, *stack), jnp.bfloat16),
             pltpu.VMEM(turned, jnp.bfloat16),
-        ),
-        in_specs=[pl.BlockSpec(memory_space=pltpu.VMEM)] * 9,
-        out_specs=[pl.BlockSpec(memory_space=pltpu.VMEM)] * 3,
-        scratch_shapes=[
-            pltpu.VMEM(stack, jnp.bfloat16),
+            dma((3, 4)),
+            dma((stages,)), dma((stages,)),
             dma((3, CHUNKS)), dma((3, CHUNKS)), dma((3, CHUNKS)), dma((3, CHUNKS)),
             dma((3, half)), dma((3, half)), dma((3, half)), dma((3, half)),
             dma((4, 3, CHUNKS)), dma((4, 3, CHUNKS)),
         ],
         compiler_params=pltpu.CompilerParams(
-            collective_id=0, has_side_effects=True, vmem_limit_bytes=20 * 2**20
+            collective_id=0, has_side_effects=True, vmem_limit_bytes=58 * 2**20
         ),
         name="gather_merged",
-    )(*sources)
-
-
-def store_kernel(gate, up, down, gate_out, up_out, down_out, sems):
-    pieces = 4
-    copies = []
-    for i, (src, dst) in enumerate(((gate, gate_out), (up, up_out), (down, down_out))):
-        size = src.shape[0] // pieces
-        for k in range(pieces):
-            at = pl.ds(k * size, size)
-            copies.append(pltpu.make_async_copy(src.at[at, :], dst.at[at, :], sems.at[i, k]))
-            copies[-1].start()
-    for copy in copies:
-        copy.wait()
-
-
-def store(gate, up, down):
-    return pl.pallas_call(
-        store_kernel,
-        out_shape=tuple(jax.ShapeDtypeStruct(a.shape, a.dtype) for a in (gate, up, down)),
-        in_specs=[pl.BlockSpec(memory_space=pltpu.VMEM)] * 3,
-        out_specs=[pl.BlockSpec(memory_space=pl.ANY)] * 3,
-        scratch_shapes=[pltpu.SemaphoreType.DMA((3, 4))],
-        compiler_params=pltpu.CompilerParams(vmem_limit_bytes=2**20),
-        name="store_merged",
-    )(gate, up, down)
+    )(*sources, *norms)
 
 
 def local(
@@ -209,24 +222,26 @@
     weight_up, low_up, high_up,
     weight_down, low_down, high_down,
     norm_train, norm_step,
-    *, fast,
+    *, fast, tp,
 ):
-    serve_norm = lax.all_gather(
-        (norm_train + norm_step).astype(jnp.bfloat16), ("zero", "tp"), axis=0, tiled=True
-    )
     sources = (
         (weight_down.T, high_down, low_down.T),
         (weight_gate, low_gate.T, high_gate),
         (weight_up, low_up.T, high_up),
     )
     if fast:
-        ready_gate, ready_up, ready_down = store(*gather(sum(sources, ()), None))
+        norms = (norm_train[None], norm_step[None])
+        ready_gate, ready_up, ready_down, gains = gather(sum(sources, ()), norms, tp)
+        serve_norm = gains[:, 0, : norm_train.shape[0]].reshape(-1).astype(jnp.bfloat16)
     else:
         down, gate, up = (merge_rows(*s) for s in sources)
         ready_gate, ready_up, ready_down = (
             lax.all_gather(a, "zero", axis=0, tiled=True) for a in (gate, up, down)
         )
         ready_down = ready_down.T
+        serve_norm = lax.all_gather(
+            (norm_train + norm_step).astype(jnp.bfloat16), ("zero", "tp"), axis=0, tiled=True
+        )
     return (ready_gate, ready_up, ready_down, serve_norm)
 
 
@@ -236,12 +251,15 @@
         rows, columns = args[0].shape[0] // zero, args[0].shape[1] // tp
         fast = (
             zero == GROUP
+            and tp & (tp - 1) == 0
+            and args[9].shape[0] <= zero * tp * LANES
             and rows % (16 * CHUNKS) == 0
             and columns % LANES == 0
+            and 2 * rows % LANES == 0
             and args[6].shape == args[0].shape[::-1]
         )
         return jax.shard_map(
-            functools.partial(local, fast=fast),
+            functools.partial(local, fast=fast, tp=tp),
             mesh=mesh,
             in_specs=(
                 P("zero", "tp"), P("zero", None), P(None, "tp"),

time: 237 us -> 199 us (0.84)
  blocking collectives: 39.6 us -> 0 us
  local copies, waits for them, and re-layouts: 18.8 us -> 27.1 us
  Pallas kernels: 177 us -> 170 us
    unnamed x1 -> x0, blocking collectives: 39.6 us -> none
    pallas_call x2 -> x1, Pallas kernels: 177 us -> 170 us  [gather(): pl.pallas_call(functools.partial(gather_kernel, tp), out_shape=(jax.Shape...]
    unnamed x14 -> x11, local copies, waits for them, and re-layouts: 18.8 us -> 25.7 us
where the time goes in v2:
time: 199 us; the launch traced here: 197 us
  Pallas kernels  170 us (85%)
  local copies, waits for them, and re-layouts  27.1 us (14%)
    pallas_call x1, Pallas kernels, gather(): pl.pallas_call(functools.partial(gather_kernel, tp), out_shape=(jax.Shape...  170 us
    unnamed x11, local copies, waits for them, and re-layouts  25.7 us

profile of v2, /device:TPU:0, one launch (start us, length us, event | category | flops | bytes accessed | tf_op | source)
XLA Modules:
  0.0 197.4 jit_solution(10787857601496103502)
XLA Ops:
  0.6 169.6 %gather_merged.1 = (bf16[2560,2432]{1,0:T(8,128)(2,1)}, bf16[2560,2432]{1,0:T(8,128)(2,1)}, bf16[2432,2560]{1,0:T(8,128)(2,1)}, f32[32,1,128]{2,1,0:T(1,128)}) custom-call(bf16[320,2432]{1,0:T(8,128)(2,1)} %bitcast.8, bf16[16,320]{1,0:T(8,128)(2,1)} %factor_down.1, bf16[16,2432]{1,0:T(8,128)(2,1)} %bitcast.9, bf16[320,2432]{1,0:T(8,128)(2,1)} %weight_gate.1, ...), custom_call_target="tpu_custom_call" | custom-call | tf_op jit(solution)/shard_map/gather_merged/pallas_call | solution.py:193
  170.3 0.8 fusion
  171.0 0.7 convert_element_type.4
  171.7 0.0 copy-start
  171.7 0.0 slice-start
  171.7 0.0 slice-start.1
  171.7 12.3 %copy.18 = bf16[2560,2432]{1,0:T(8,128)(2,1)} copy(bf16[2560,2432]{1,0:T(8,128)(2,1)} %get-tuple-element.16) | data formatting | bytes 24903680
  184.0 0.0 copy-done
  184.0 0.0 slice-start.2
  184.0 6.3 %copy.19 = bf16[2560,2432]{1,0:T(8,128)(2,1)} copy(bf16[2560,2432]{1,0:T(8,128)(2,1)S(1)} %copy-done) | data formatting | bytes 24903680
  190.3 0.0 slice-done
  190.3 1.0 slice-done.1
  191.4 1.3 slice-done.2
  192.7 4.7 %copy.20 = bf16[2432,2560]{1,0:T(8,128)(2,1)} copy(bf16[2432,2560]{1,0:T(8,128)(2,1)S(1)} %bitcast.7) | data formatting | bytes 24903680
  (1 shorter events, 0.0 us)
Async XLA Ops:
  171.7 12.3 %copy-start = (bf16[2560,2432]{1,0:T(8,128)(2,1)S(1)}, bf16[2560,2432]{1,0:T(8,128)(2,1)}, u32[]{:S(2)}) copy-start(bf16[2560,2432]{1,0:T(8,128)(2,1)} %get-tuple-element.17) | copy-start | bytes 37355524
  171.7 18.6 %slice-start = ((s8[12451840]{0:T(1024)(128)(4,1)}), s8[4194304]{0:T(1024)(128)(4,1)S(1)}, s32[]{:S(2)}) async-start(s8[12451840]{0:T(1024)(128)(4,1)} %bitcast.6), calls=%async_computation | async-start | bytes 8388608
  171.7 19.7 %slice-start.1 = ((s8[12451840]{0:T(1024)(128)(4,1)}), s8[4194304]{0:T(1024)(128)(4,1)S(1)}, s32[]{:S(2)}) async-start(s8[12451840]{0:T(1024)(128)(4,1)} %bitcast.6), calls=%async_computation.1 | async-start | bytes 8388608
  184.0 8.6 %slice-start.2 = ((s8[12451840]{0:T(1024)(128)(4,1)}), s8[4063232]{0:T(1024)(128)(4,1)S(1)}, s32[]{:S(2)}) async-start(s8[12451840]{0:T(1024)(128)(4,1)} %bitcast.6), calls=%async_computation.2 | async-start | bytes 8126464

commit v3 on v1

--- a/solution.py
+++ b/solution.py
@@ -12,6 +12,7 @@
 LANES = 128
 CHUNKS = 4
 GROUP = 8
+GRANT = 20 * 2**20
 
 
 def merge_rows(weight, factor, other):
@@ -22,10 +23,13 @@
 
 
 def gather_kernel(
+    tp,
     weight_down, factor_down, other_down,
     weight_gate, factor_gate, other_gate,
     weight_up, factor_up, other_up,
-    gate, up, down, held,
+    norm_train, norm_step,
+    gate, up, down, gains, held, weights, w_sems,
+    n_send, n_recv,
     x_send, x_recv, y_send, y_recv, fx_send, fx_recv, fy_send, fy_recv, p_send, p_recv,
 ):
     rows, columns = weight_gate.shape
@@ -44,16 +48,50 @@
     across_y = at(1 - y, x, core)
     across = at(1 - y, 1 - x, core)
 
+    loads = [
+        pltpu.make_async_copy(weight, weights.at[i], w_sems.at[i])
+        for i, weight in enumerate((weight_down, weight_gate, weight_up))
+    ]
+    for load in loads:
+        load.start()
+
+    mine = lax.axis_index("tp")
+    group = [
+        at(
+            y + dy - 2 * y * dy,
+            x + dx - 2 * x * dx,
+            core + dc - 2 * core * dc,
+        )
+        for dy in (0, 1) for dx in (0, 1) for dc in (0, 1) if dy + dx + dc
+    ]
+    peers, width = [{"zero": peer} for peer in group], 1
+    while width < tp:
+        bit = lax.rem(lax.div(mine, width), 2)
+        peers.append({"tp": mine + width - 2 * width * bit})
+        width *= 2
+
     barrier = pltpu.get_barrier_semaphore()
-    for peer in (partner, across_x, across_y):
-        pl.semaphore_signal(barrier, inc=1, device_id={"zero": peer}, device_id_type=MESH)
-    pl.semaphore_wait(barrier, 3)
+    for peer in peers:
+        pl.semaphore_signal(barrier, inc=1, device_id=peer, device_id_type=MESH)
+    place = mine * GROUP + me
+    size = norm_train.shape[1]
+    gains[place, :, 0:size] = norm_train[...] + norm_step[...]
+    pl.semaphore_wait(barrier, len(peers))
+
+    def pass_gains(k, first, count):
+        block = gains.at[pl.ds(first, count)]
+        dma = pltpu.make_async_remote_copy(
+            src_ref=block, dst_ref=block, send_sem=n_send.at[k], recv_sem=n_recv.at[k],
+            device_id=peers[k], device_id_type=MESH,
+        )
+        dma.start()
+        return dma
+
+    passed = [pass_gains(k, place, 1) for k in range(len(group))]
 
     stacks = (held, gate, up)
-    sources = (
-        (weight_down, factor_down, other_down),
-        (weight_gate, factor_gate, other_gate),
-        (weight_up, factor_up, other_up),
+    factors = (
+        (factor_down, other_down), (factor_gate, other_gate), (factor_up, other_up)
     )
 
     def part(i, owner, c, count=1):
@@ -90,14 +128,15 @@
         sent.append(dma)
 
     for i in range(3):
-        weight, factor, other = sources[i]
+        factor, other = factors[i]
+        loads[i].wait()
         first = pl.multiple_of(me * rows, 16)
 
         @pl.loop(0, columns // LANES)
         def _(t):
             cols = pl.ds(pl.multiple_of(t * LANES, LANES), LANES)
             stacks[i][pl.ds(first, rows), cols] = merge_rows(
-                weight[:, cols], factor[...], other[:, cols]
+                weights[i, :, cols], factor[...], other[:, cols]
             )
 
         for cx, cy in zip((*early, *late), (*late, *early)):
@@ -105,6 +144,14 @@
             go(on_y(i, me, cy))
         for c in range(CHUNKS):
             go(share(i, 0, me, c))
+
+    for dma in passed:
+        dma.wait_recv()
+    for k in range(len(group), len(peers)):
+        width = 1 << (k - len(group))
+        passed.append(pass_gains(k, lax.div(mine, width) * (width * GROUP), width * GROUP))
+        passed[-1].wait_recv()
+    sent += passed
 
     def turn(owner):
         base = pl.multiple_of(lax.div(owner, 2) * (2 * rows), LANES)
@@ -151,37 +198,45 @@
         dma.wait_send()
 
 
-def gather(sources, names):
+def gather(sources, norms, tp):
     rows, columns = sources[0].shape
     stack = (rows * GROUP, columns)
     turned = (columns, rows * GROUP)
     dma = pltpu.SemaphoreType.DMA
     half = CHUNKS // 2
+    stages = GROUP - 1 + tp.bit_length() - 1
+    anywhere = pl.BlockSpec(memory_space=pl.ANY)
+    held = pl.BlockSpec(memory_space=pltpu.VMEM)
     return pl.pallas_call(
-        gather_kernel,
+        functools.partial(gather_kernel, tp),
         out_shape=(
             pltpu.VMEM(stack, jnp.bfloat16),
             pltpu.VMEM(stack, jnp.bfloat16),
             pltpu.VMEM(turned, jnp.bfloat16),
+            pltpu.VMEM((GROUP * tp, 1, LANES), jnp.float32),
         ),
-        in_specs=[pl.BlockSpec(memory_space=pltpu.VMEM)] * 9,
-        out_specs=[pl.BlockSpec(memory_space=pltpu.VMEM)] * 3,
+        in_specs=[anywhere, held, held] * 3 + [held, held],
+        out_specs=[pl.BlockSpec(memory_space=pltpu.VMEM)] * 4,
         scratch_shapes=[
             pltpu.VMEM(stack, jnp.bfloat16),
+            pltpu.VMEM((3, rows, columns), jnp.bfloat16),
+            dma((3,)),
+            dma((stages,)), dma((stages,)),
             dma((3, CHUNKS)), dma((3, CHUNKS)), dma((3, CHUNKS)), dma((3, CHUNKS)),
             dma((3, half)), dma((3, half)), dma((3, half)), dma((3, half)),
             dma((4, 3, CHUNKS)), dma((4, 3, CHUNKS)),
         ],
         compiler_params=pltpu.CompilerParams(
-            collective_id=0, has_side_effects=True, vmem_limit_bytes=20 * 2**20
+            collective_id=0, has_side_effects=True, vmem_limit_bytes=GRANT
         ),
         name="gather_merged",
-    )(*sources)
-
-
-def store_kernel(gate, up, down, gate_out, up_out, down_out, sems):
+    )(*sources, *norms)
+
+
+def store_kernel(gate, up, down, gains, gate_out, up_out, down_out, gains_out, sems):
     pieces = 4
-    copies = []
+    copies = [pltpu.make_async_copy(gains, gains_out, sems.at[3, 0])]
+    copies[0].start()
     for i, (src, dst) in enumerate(((gate, gate_out), (up, up_out), (down, down_out))):
         size = src.shape[0] // pieces
         for k in range(pieces):
@@ -192,16 +247,17 @@
         copy.wait()
 
 
-def store(gate, up, down):
+def store(*held):
+    held = [pltpu.with_memory_space_constraint(a, pltpu.VMEM) for a in held]
     return pl.pallas_call(
         store_kernel,
-        out_shape=tuple(jax.ShapeDtypeStruct(a.shape, a.dtype) for a in (gate, up, down)),
-        in_specs=[pl.BlockSpec(memory_space=pltpu.VMEM)] * 3,
-        out_specs=[pl.BlockSpec(memory_space=pl.ANY)] * 3,
-        scratch_shapes=[pltpu.SemaphoreType.DMA((3, 4))],
-        compiler_params=pltpu.CompilerParams(vmem_limit_bytes=2**20),
+        out_shape=tuple(jax.ShapeDtypeStruct(a.shape, a.dtype) for a in held),
+        in_specs=[pl.BlockSpec(memory_space=pltpu.VMEM)] * 4,
+        out_specs=[pl.BlockSpec(memory_space=pl.ANY)] * 4,
+        scratch_shapes=[pltpu.SemaphoreType.DMA((4, 4))],
+        compiler_params=pltpu.CompilerParams(vmem_limit_bytes=GRANT),
         name="store_merged",
-    )(gate, up, down)
+    )(*held)
 
 
 def local(
@@ -209,24 +265,27 @@
     weight_up, low_up, high_up,
     weight_down, low_down, high_down,
     norm_train, norm_step,
-    *, fast,
+    *, fast, tp,
 ):
-    serve_norm = lax.all_gather(
-        (norm_train + norm_step).astype(jnp.bfloat16), ("zero", "tp"), axis=0, tiled=True
-    )
     sources = (
         (weight_down.T, high_down, low_down.T),
         (weight_gate, low_gate.T, high_gate),
         (weight_up, low_up.T, high_up),
     )
     if fast:
-        ready_gate, ready_up, ready_down = store(*gather(sum(sources, ()), None))
+        norms = (norm_train[None], norm_step[None])
+        ready_gate, ready_up, ready_down, gains = store(*gather(sum(sources, ()), norms, tp))
+        gains = gains[:, 0, : norm_train.shape[0]].reshape(tp, GROUP, -1)
+        serve_norm = gains.transpose(1, 0, 2).reshape(-1).astype(jnp.bfloat16)
     else:
         down, gate, up = (merge_rows(*s) for s in sources)
         ready_gate, ready_up, ready_down = (
             lax.all_gather(a, "zero", axis=0, tiled=True) for a in (gate, up, down)
         )
         ready_down = ready_down.T
+        serve_norm = lax.all_gather(
+            (norm_train + norm_step).astype(jnp.bfloat16), ("zero", "tp"), axis=0, tiled=True
+        )
     return (ready_gate, ready_up, ready_down, serve_norm)
 
 
@@ -236,12 +295,15 @@
         rows, columns = args[0].shape[0] // zero, args[0].shape[1] // tp
         fast = (
             zero == GROUP
+            and tp & (tp - 1) == 0
+            and args[9].shape[0] <= zero * tp * LANES
             and rows % (16 * CHUNKS) == 0
             and columns % LANES == 0
+            and 2 * rows % LANES == 0
             and args[6].shape == args[0].shape[::-1]
         )
         return jax.shard_map(
-            functools.partial(local, fast=fast),
+            functools.partial(local, fast=fast, tp=tp),
             mesh=mesh,
             in_specs=(
                 P("zero", "tp"), P("zero", None), P(None, "tp"),

time: 237 us -> 179 us (0.76)
  blocking collectives: 39.6 us -> 0 us
  local copies, waits for them, and re-layouts: 18.8 us -> 1.42 us
    unnamed x1 -> x0, blocking collectives: 39.6 us -> none
    unnamed x14 -> x1, local copies, waits for them, and re-layouts: 18.8 us -> 0.01 us
where the time goes in v3:
time: 179 us
  Pallas kernels  177 us (99%)
    pallas_call x1, Pallas kernels, gather(): pl.pallas_call(functools.partial(gather_kernel, tp), out_shape=(pltpu.VME...  165 us
    pallas_call x1, Pallas kernels, store(): pl.pallas_call(store_kernel, out_shape=tuple((jax.ShapeDtypeStruct(a.shap...  12.3 us

profile of v3, /device:TPU:0, one launch (start us, length us, event | category | flops | bytes accessed | tf_op | source)
XLA Modules:
  0.0 179.1 jit_solution(12378063369859211282)
XLA Ops:
  0.6 164.8 %gather_merged.1 = (bf16[2560,2432]{1,0:T(8,128)(2,1)S(1)}, bf16[2560,2432]{1,0:T(8,128)(2,1)S(1)}, bf16[2432,2560]{1,0:T(8,128)(2,1)S(1)}, f32[32,1,128]{2,1,0:T(1,128)S(1)}) custom-call(bf16[320,2432]{1,0:T(8,128)(2,1)} %bitcast.11, bf16[16,320]{1,0:T(8,128)(2,1)} %factor_down.1, bf16[16,2432]{1,0:T(8,128)(2,1)} %bitcast.12, ...), custom_call_target="tpu_custom_call" | custom-call | tf_op jit(solution)/shard_map/gather_merged/pallas_call | solution.py:210
  165.4 12.3 %store_merged.1 = (bf16[2560,2432]{1,0:T(8,128)(2,1)}, bf16[2560,2432]{1,0:T(8,128)(2,1)}, bf16[2432,2560]{1,0:T(8,128)(2,1)}, f32[32,1,128]{2,1,0:T(1,128)}) custom-call(bf16[2560,2432]{1,0:T(8,128)(2,1)S(1)} %get-tuple-element.12.gate, bf16[2560,2432]{1,0:T(8,128)(2,1)S(1)} %get-tuple-element.13.up, bf16[2432,2560]{1,0:T(8,128)(2,1)S(1)} %get-tuple-element.14.down, ...), custom_call_target="tpu_custom_call" | custom-call | tf_op jit(solution)/shard_map/store_merged/pallas_call | solution.py:252
  177.7 0.7 slice.7
  178.4 0.7 convert_element_type.12
  (2 shorter events, 0.0 us)
